TPU v7x, 32 devices: a whole 2x2x4 slice. The times are simulated.
32 devices in a mesh: gx: 2 (over x), gy: 4 (over z), gz: 4 (over y, core).
Axes of the slice: x: 2, y: 2, z: 4, core: 2. Of those that a mesh axis runs over, the one named last changes fastest.
Arguments:
- partials: float32 [32, 32, 64, 512], P('gx', None, 'gy', 'gz'), may hold values from -40 to 40
- code_bits: int32 [32, 32], replicated, may hold values from 0 to 1
- group_map: int32 [32], replicated, may hold values from 0 to 31, each once
- velocity: float32 [32, 64, 512], P('gx', 'gy', 'gz'), may hold values from 1.5 to 4.5
Outputs:
- gradient: float32 [32, 64, 512], P('gx', 'gy', 'gz')
- new_model: float32 [32, 64, 512], P('gx', 'gy', 'gz')
Inputs may be any that keep to these rules, and one draw needn't show every extreme that they name: `group_map`: every group of 0 to 31 stands in exactly one slot.
All inputs are finite; a program needn't handle non-finite values.
Results may differ from a plain program's by a relative error of at most 0.0001.
Values sent between devices are 32-bit elements; how exact they have to be, the bound alone decides.
A program may use at most 64 MiB of HBM per device.

v0:
```python
import jax
import jax.numpy as jnp
from jax import lax
from jax.sharding import PartitionSpec as P

ITERS = 3


step_length = 0.5
tv_weight = 0.2
dual_step = 0.28
primal_step = 0.28


def from_behind(block, axis, distance):
    devices = range(lax.axis_size(axis))
    route = [(i - distance, i) for i in devices if i - distance in devices]
    return lax.ppermute(block, axis, route)


def edge_mask(position, count, length, shape):
    global_index = position * length + jnp.arange(length, dtype=jnp.int32)
    keep = (global_index < count * length - 1).astype(jnp.float32)
    return keep.reshape(shape)


def neighbours_after(extra):
    next_x = jnp.concatenate([extra[1:], from_behind(extra[:1], "gx", -1)], 0)
    next_y = jnp.concatenate([extra[:, 1:], from_behind(extra[:, :1], "gy", -1)], 1)
    next_z = jnp.concatenate([extra[:, :, 1:], from_behind(extra[:, :, :1], "gz", -1)], 2)
    return (next_x, next_y, next_z)


def neighbours_before(dual_field):
    before_x = jnp.concatenate([from_behind(dual_field[0, -1:], "gx", 1), dual_field[0, :-1]], 0)
    before_y = jnp.concatenate(
        [from_behind(dual_field[1, :, -1:], "gy", 1), dual_field[1, :, :-1]], 1
    )
    before_z = jnp.concatenate(
        [from_behind(dual_field[2, :, :, -1:], "gz", 1), dual_field[2, :, :, :-1]], 2
    )
    return (before_x, before_y, before_z)


def shards(partials, code_bits, group_map, velocity):
    slot_count = partials.shape[0]
    groups = group_map.shape[0]
    block_x, block_y, block_z = velocity.shape
    onehot = (group_map[:, None] == jnp.arange(groups, dtype=jnp.int32)[None, :]).astype(
        jnp.float32
    )
    slot_bits = jnp.dot(onehot, code_bits.astype(jnp.float32), precision=lax.Precision.HIGHEST)
    sign_table = 2.0 * slot_bits - 1.0
    own_signs = lax.dynamic_slice_in_dim(
        sign_table, lax.axis_index("gx") * slot_count, slot_count, 0
    )
    gradient = lax.psum_scatter(
        jnp.einsum("gx,gxyz->xyz", own_signs, partials, precision=lax.Precision.HIGHEST),
        "gx",
        scatter_dimension=0,
        tiled=True,
    )
    square_sum = lax.psum(jnp.sum(gradient * gradient), ("gx", "gy", "gz"))
    cell_count = (
        block_x
        * block_y
        * block_z
        * lax.axis_size("gx")
        * lax.axis_size("gy")
        * lax.axis_size("gz")
    )
    step_scale = step_length / jnp.sqrt(square_sum / cell_count + 1.0)
    target = velocity - step_scale * gradient
    mask_x = edge_mask(lax.axis_index("gx"), lax.axis_size("gx"), block_x, (block_x, 1, 1))
    mask_y = edge_mask(lax.axis_index("gy"), lax.axis_size("gy"), block_y, (1, block_y, 1))
    mask_z = edge_mask(lax.axis_index("gz"), lax.axis_size("gz"), block_z, (1, 1, block_z))
    current = target
    extra = target
    dual_field = jnp.zeros((3,) + target.shape, jnp.float32)
    for iteration in range(ITERS):
        next_x, next_y, next_z = neighbours_after(extra)
        differences = jnp.stack(
            [(next_x - extra) * mask_x, (next_y - extra) * mask_y, (next_z - extra) * mask_z]
        )
        dual_field = dual_field + dual_step * differences
        magnitude = jnp.sqrt(jnp.sum(dual_field * dual_field, axis=0))
        dual_field = dual_field / jnp.maximum(1.0, magnitude / tv_weight)[None]
        before_x, before_y, before_z = neighbours_before(dual_field)
        spread = dual_field[0] - before_x + (dual_field[1] - before_y) + (dual_field[2] - before_z)
        updated = (current + primal_step * spread + primal_step * target) / (1.0 + primal_step)
        extra = 2.0 * updated - current
        current = updated
    return (gradient, current)


def solution(mesh):
    placed = (P("gx", None, "gy", "gz"), P(), P(), P("gx", "gy", "gz"))
    return jax.shard_map(
        shards,
        mesh=mesh,
        in_specs=placed,
        out_specs=(P("gx", "gy", "gz"), P("gx", "gy", "gz")),
        check_vma=False,
    )
```

profile of v0, /device:TPU:0, one launch (start us, length us, event | category | flops | bytes accessed | tf_op | source)
XLA Modules:
  0.0 149.6 jit_solution(10523836130631386488)
XLA Ops:
  7.2 0.9 fusion.48
  8.2 6.4 %fusion = f32[32,1,16,128]{3,1,2,0:T(1,128)S(1)} fusion(f32[16,32,1,1]{0,2,3,1:T(1,128)S(1)} %copy.33, f32[16,32,16,128]{3,2,1,0:T(8,128)} %param.4), kind=kOutput, calls=%fused_computation | convolution fusion | flops 12582912 | bytes 4458496 | tf_op jit(solution)/shard_map/gx,gxyz->xyz/dot_general | solution.py:58
  14.7 0.8 copy.43
  15.5 14.6 %reduce-scatter.2.cloned.1.call-done = f32[16,16,128]{2,0,1:T(8,128)} async-done(((f32[32,16,128]{2,0,1:T(8,128)}), f32[16,16,128]{2,0,1:T(8,128)}) %reduce-scatter.2.cloned.1.call-update) | async-done | bytes 131088 | tf_op jit(solution)/shard_map/reduce_scatter | solution.py:57
  30.1 1.5 %multiply_reduce_fusion.3 = f32[]{:T(128)} fusion(f32[16,16,128]{2,0,1:T(8,128)} %reduce-scatter.2.cloned.1.call-done), kind=kLoop, calls=%fused_computation.87 | loop fusion | flops 65535 | bytes 131076 | tf_op jit(solution)/shard_map/reduce_sum | solution.py:63
  31.7 39.5 %psum.7 = f32[]{:T(128)} all-reduce(f32[]{:T(128)} %multiply_reduce_fusion.3), channel_id=1, replica_groups=mesh['gx'=2,'gy'=4,'gz'=4] {'gx','gy','gz'}, use_global_device_ids=true, to_apply=%region_2.0 | all-reduce | flops 1 | bytes 8 | tf_op jit(solution)/shard_map/psum | solution.py:63
  71.9 1.0 copy_subtract_fusion
  72.8 1.3 collective-permute-start
  74.1 1.3 collective-permute-start.1
  75.4 1.3 collective-permute-start.2
  76.9 1.8 %collective-permute-done.2 = f32[16,16,1]{2,0,1:T(8,128)S(1)} collective-permute-done((f32[16,16,1]{2,0,1:T(8,128)S(1)}, f32[16,16,1]{2,0,1:T(8,128)S(1)}, u32[]{:S(2)}, u32[]{:S(2)}) %collective-permute-start.2) | collective-permute-done | bytes 1056 | tf_op jit(solution)/shard_map/ppermute | solution.py:18
  78.7 1.0 collective-permute-done.1
  80.1 4.5 %collective-permute-start.3 = (f32[1,16,128]{2,0,1:T(1,128)S(1)}, f32[1,16,128]{2,0,1:T(1,128)S(1)}, u32[]{:S(2)}, u32[]{:S(2)}) collective-permute-start(f32[1,16,128]{2,0,1:T(1,128)S(1)} %slice_bitcast_fusion.23), channel_id=1, source_target_pairs={{0,16},{1,17},{2,18},{3,19},{4,20},{5,21},{6,22},{7,23},{8,24},{9,... | collective-permute-start | bytes 24584 | tf_op jit(solution)/shard_map/ppermute | solution.py:18
  84.7 3.6 %collective-permute-start.4 = (f32[16,1,128]{2,0,1:T(8,128)S(1)}, f32[16,1,128]{2,0,1:T(8,128)S(1)}, u32[]{:S(2)}, u32[]{:S(2)}) collective-permute-start(f32[16,1,128]{2,0,1:T(8,128)S(1)} %slice_bitcast_fusion.22), channel_id=1, source_target_pairs={{0,4},{4,8},{8,12},{1,5},{5,9},{9,13},{2,6},{6,10},{10,14},{3,7},{... | collective-permute-start | bytes 24584 | tf_op jit(solution)/shard_map/ppermute | solution.py:18
  88.6 5.2 %collective-permute-start.5 = (f32[16,16,1]{2,0,1:T(8,128)S(1)}, f32[16,16,1]{2,0,1:T(8,128)S(1)}, u32[]{:S(2)}, u32[]{:S(2)}) collective-permute-start(f32[16,16,1]{2,0,1:T(8,128)S(1)} %copy.24), channel_id=1, source_target_pairs={{0,1},{1,2},{2,3},{4,5},{5,6},{6,7},{8,9},{9,10},{10,11},{12,13},{... | collective-permute-start | bytes 3080 | tf_op jit(solution)/shard_map/ppermute | solution.py:18
  93.9 0.9 collective-permute-done.5
  95.0 1.3 collective-permute-start.6
  96.3 1.3 collective-permute-start.7
  97.6 1.3 collective-permute-start.8
  99.0 2.7 %collective-permute-done.8 = f32[16,16,1]{2,0,1:T(8,128)S(1)} collective-permute-done((f32[16,16,1]{2,0,1:T(8,128)S(1)}, f32[16,16,1]{2,0,1:T(8,128)S(1)}, u32[]{:S(2)}, u32[]{:S(2)}) %collective-permute-start.8) | collective-permute-done | bytes 1056 | tf_op jit(solution)/shard_map/ppermute | solution.py:18
  102.4 4.5 %collective-permute-start.9 = (f32[1,16,128]{2,0,1:T(1,128)S(1)}, f32[1,16,128]{2,0,1:T(1,128)S(1)}, u32[]{:S(2)}, u32[]{:S(2)}) collective-permute-start(f32[1,16,128]{2,0,1:T(1,128)S(1)} %slice_bitcast_fusion.21), channel_id=1, source_target_pairs={{0,16},{1,17},{2,18},{3,19},{4,20},{5,21},{6,22},{7,23},{8,24},{9,... | collective-permute-start | bytes 24584 | tf_op jit(solution)/shard_map/ppermute | solution.py:18
  106.9 3.9 %collective-permute-start.10 = (f32[16,1,128]{2,0,1:T(8,128)S(1)}, f32[16,1,128]{2,0,1:T(8,128)S(1)}, u32[]{:S(2)}, u32[]{:S(2)}) collective-permute-start(f32[16,1,128]{2,0,1:T(8,128)S(1)} %slice_bitcast_fusion.20), channel_id=1, source_target_pairs={{0,4},{4,8},{8,12},{1,5},{5,9},{9,13},{2,6},{6,10},{10,14},{3,7},{... | collective-permute-start | bytes 24584 | tf_op jit(solution)/shard_map/ppermute | solution.py:18
  111.2 6.2 %collective-permute-start.11 = (f32[16,16,1]{2,0,1:T(8,128)S(1)}, f32[16,16,1]{2,0,1:T(8,128)S(1)}, u32[]{:S(2)}, u32[]{:S(2)}) collective-permute-start(f32[16,16,1]{2,0,1:T(8,128)S(1)} %copy.27), channel_id=1, source_target_pairs={{0,1},{1,2},{2,3},{4,5},{5,6},{6,7},{8,9},{9,10},{10,11},{12,13},{... | collective-permute-start | bytes 3080 | tf_op jit(solution)/shard_map/ppermute | solution.py:18
  117.4 0.9 collective-permute-done.11
  118.5 1.3 collective-permute-start.12
  119.8 1.3 collective-permute-start.13
  121.1 1.3 collective-permute-start.14
  123.2 2.0 %collective-permute-done.14 = f32[16,16,1]{2,0,1:T(8,128)S(1)} collective-permute-done((f32[16,16,1]{2,0,1:T(8,128)S(1)}, f32[16,16,1]{2,0,1:T(8,128)S(1)}, u32[]{:S(2)}, u32[]{:S(2)}) %collective-permute-start.14) | collective-permute-done | bytes 1056 | tf_op jit(solution)/shard_map/ppermute | solution.py:18
  125.9 4.5 %collective-permute-start.15 = (f32[1,16,128]{2,0,1:T(1,128)S(1)}, f32[1,16,128]{2,0,1:T(1,128)S(1)}, u32[]{:S(2)}, u32[]{:S(2)}) collective-permute-start(f32[1,16,128]{2,0,1:T(1,128)S(1)} %slice_bitcast_fusion.19), channel_id=1, source_target_pairs={{0,16},{1,17},{2,18},{3,19},{4,20},{5,21},{6,22},{7,23},{8,24},{9,... | collective-permute-start | bytes 24584 | tf_op jit(solution)/shard_map/ppermute | solution.py:18
  130.5 3.9 %collective-permute-start.16 = (f32[16,1,128]{2,0,1:T(8,128)S(1)}, f32[16,1,128]{2,0,1:T(8,128)S(1)}, u32[]{:S(2)}, u32[]{:S(2)}) collective-permute-start(f32[16,1,128]{2,0,1:T(8,128)S(1)} %slice_bitcast_fusion.18), channel_id=1, source_target_pairs={{0,4},{4,8},{8,12},{1,5},{5,9},{9,13},{2,6},{6,10},{10,14},{3,7},{... | collective-permute-start | bytes 24584 | tf_op jit(solution)/shard_map/ppermute | solution.py:18
  134.8 6.2 %collective-permute-start.17 = (f32[16,16,1]{2,0,1:T(8,128)S(1)}, f32[16,16,1]{2,0,1:T(8,128)S(1)}, u32[]{:S(2)}, u32[]{:S(2)}) collective-permute-start(f32[16,16,1]{2,0,1:T(8,128)S(1)} %copy.30), channel_id=1, source_target_pairs={{0,1},{1,2},{2,3},{4,5},{5,6},{6,7},{8,9},{9,10},{10,11},{12,13},{... | collective-permute-start | bytes 3080 | tf_op jit(solution)/shard_map/ppermute | solution.py:18
  140.9 0.9 collective-permute-done.17
  (77 shorter events, 5.0 us)
Async XLA Ops:
  7.2 64.7 %copy-start.1 = (f32[16,16,128]{2,1,0:T(8,128)S(1)}, f32[16,16,128]{2,1,0:T(8,128)}, u32[]{:S(2)}) copy-start(f32[16,16,128]{2,1,0:T(8,128)} %param.7) | copy-start | bytes 393220
  7.2 23.0 %reduce-scatter.2.cloned.1.call-start = ((), (), s32[]{:S(2)}) async-start(), calls=%async_computation.1 | async-start | bytes 393216 | tf_op jit(solution)/shard_map/reduce_scatter | solution.py:57
  72.8 5.8 %collective-permute-start = (f32[1,16,128]{2,0,1:T(1,128)S(1)}, f32[1,16,128]{2,0,1:T(1,128)S(1)}, u32[]{:S(2)}, u32[]{:S(2)}) collective-permute-start(f32[1,16,128]{2,0,1:T(1,128)S(1)} %slice.181), channel_id=1, source_target_pairs={{16,0},{17,1},{18,2},{19,3},{20,4},{21,5},{22,6},{23,7},{24,8},{25... | collective-permute-start | bytes 24584 | tf_op jit(solution)/shard_map/ppermute | solution.py:18
  74.1 5.5 %collective-permute-start.1 = (f32[16,1,128]{2,0,1:T(8,128)S(1)}, f32[16,1,128]{2,0,1:T(8,128)S(1)}, u32[]{:S(2)}, u32[]{:S(2)}) collective-permute-start(f32[16,1,128]{2,0,1:T(8,128)S(1)} %slice.183), channel_id=1, source_target_pairs={{4,0},{8,4},{12,8},{5,1},{9,5},{13,9},{6,2},{10,6},{14,10},{7,3},{... | collective-permute-start | bytes 24584 | tf_op jit(solution)/shard_map/ppermute | solution.py:18
  75.4 3.2 %collective-permute-start.2 = (f32[16,16,1]{2,0,1:T(8,128)S(1)}, f32[16,16,1]{2,0,1:T(8,128)S(1)}, u32[]{:S(2)}, u32[]{:S(2)}) collective-permute-start(f32[16,16,1]{2,0,1:T(8,128)S(1)} %bitcast.152), channel_id=1, source_target_pairs={{1,0},{2,1},{3,2},{5,4},{6,5},{7,6},{9,8},{10,9},{11,10},{13,12},{... | collective-permute-start | bytes 3080 | tf_op jit(solution)/shard_map/ppermute | solution.py:18
  80.1 14.7 %collective-permute-start.3 = (f32[1,16,128]{2,0,1:T(1,128)S(1)}, f32[1,16,128]{2,0,1:T(1,128)S(1)}, u32[]{:S(2)}, u32[]{:S(2)}) collective-permute-start(f32[1,16,128]{2,0,1:T(1,128)S(1)} %slice_bitcast_fusion.23), channel_id=1, source_target_pairs={{0,16},{1,17},{2,18},{3,19},{4,20},{5,21},{6,22},{7,23},{8,24},{9,... | collective-permute-start | bytes 24584 | tf_op jit(solution)/shard_map/ppermute | solution.py:18
  84.7 10.1 %collective-permute-start.4 = (f32[16,1,128]{2,0,1:T(8,128)S(1)}, f32[16,1,128]{2,0,1:T(8,128)S(1)}, u32[]{:S(2)}, u32[]{:S(2)}) collective-permute-start(f32[16,1,128]{2,0,1:T(8,128)S(1)} %slice_bitcast_fusion.22), channel_id=1, source_target_pairs={{0,4},{4,8},{8,12},{1,5},{5,9},{9,13},{2,6},{6,10},{10,14},{3,7},{... | collective-permute-start | bytes 24584 | tf_op jit(solution)/shard_map/ppermute | solution.py:18
  88.6 6.2 %collective-permute-start.5 = (f32[16,16,1]{2,0,1:T(8,128)S(1)}, f32[16,16,1]{2,0,1:T(8,128)S(1)}, u32[]{:S(2)}, u32[]{:S(2)}) collective-permute-start(f32[16,16,1]{2,0,1:T(8,128)S(1)} %copy.24), channel_id=1, source_target_pairs={{0,1},{1,2},{2,3},{4,5},{5,6},{6,7},{8,9},{9,10},{10,11},{12,13},{... | collective-permute-start | bytes 3080 | tf_op jit(solution)/shard_map/ppermute | solution.py:18
  93.9 28.5 %copy-start = (f32[16,16,128]{2,0,1:T(8,128)S(1)}, f32[16,16,128]{2,0,1:T(8,128)}, u32[]{:S(2)}) copy-start(f32[16,16,128]{2,0,1:T(8,128)} %reduce-scatter.2.cloned.1.call-done) | copy-start | bytes 393220
  95.0 6.7 %collective-permute-start.6 = (f32[1,16,128]{2,0,1:T(1,128)S(1)}, f32[1,16,128]{2,0,1:T(1,128)S(1)}, u32[]{:S(2)}, u32[]{:S(2)}) collective-permute-start(f32[1,16,128]{2,0,1:T(1,128)S(1)} %slice.196), channel_id=1, source_target_pairs={{16,0},{17,1},{18,2},{19,3},{20,4},{21,5},{22,6},{23,7},{24,8},{25... | collective-permute-start | bytes 24584 | tf_op jit(solution)/shard_map/ppermute | solution.py:18
  96.3 5.5 %collective-permute-start.7 = (f32[16,1,128]{2,0,1:T(8,128)S(1)}, f32[16,1,128]{2,0,1:T(8,128)S(1)}, u32[]{:S(2)}, u32[]{:S(2)}) collective-permute-start(f32[16,1,128]{2,0,1:T(8,128)S(1)} %slice.198), channel_id=1, source_target_pairs={{4,0},{8,4},{12,8},{5,1},{9,5},{13,9},{6,2},{10,6},{14,10},{7,3},{... | collective-permute-start | bytes 24584 | tf_op jit(solution)/shard_map/ppermute | solution.py:18
  97.6 4.1 %collective-permute-start.8 = (f32[16,16,1]{2,0,1:T(8,128)S(1)}, f32[16,16,1]{2,0,1:T(8,128)S(1)}, u32[]{:S(2)}, u32[]{:S(2)}) collective-permute-start(f32[16,16,1]{2,0,1:T(8,128)S(1)} %bitcast.153), channel_id=1, source_target_pairs={{1,0},{2,1},{3,2},{5,4},{6,5},{7,6},{9,8},{10,9},{11,10},{13,12},{... | collective-permute-start | bytes 3080 | tf_op jit(solution)/shard_map/ppermute | solution.py:18
  102.4 15.9 %collective-permute-start.9 = (f32[1,16,128]{2,0,1:T(1,128)S(1)}, f32[1,16,128]{2,0,1:T(1,128)S(1)}, u32[]{:S(2)}, u32[]{:S(2)}) collective-permute-start(f32[1,16,128]{2,0,1:T(1,128)S(1)} %slice_bitcast_fusion.21), channel_id=1, source_target_pairs={{0,16},{1,17},{2,18},{3,19},{4,20},{5,21},{6,22},{7,23},{8,24},{9,... | collective-permute-start | bytes 24584 | tf_op jit(solution)/shard_map/ppermute | solution.py:18
  106.9 11.4 %collective-permute-start.10 = (f32[16,1,128]{2,0,1:T(8,128)S(1)}, f32[16,1,128]{2,0,1:T(8,128)S(1)}, u32[]{:S(2)}, u32[]{:S(2)}) collective-permute-start(f32[16,1,128]{2,0,1:T(8,128)S(1)} %slice_bitcast_fusion.20), channel_id=1, source_target_pairs={{0,4},{4,8},{8,12},{1,5},{5,9},{9,13},{2,6},{6,10},{10,14},{3,7},{... | collective-permute-start | bytes 24584 | tf_op jit(solution)/shard_map/ppermute | solution.py:18
  111.2 7.1 %collective-permute-start.11 = (f32[16,16,1]{2,0,1:T(8,128)S(1)}, f32[16,16,1]{2,0,1:T(8,128)S(1)}, u32[]{:S(2)}, u32[]{:S(2)}) collective-permute-start(f32[16,16,1]{2,0,1:T(8,128)S(1)} %copy.27), channel_id=1, source_target_pairs={{0,1},{1,2},{2,3},{4,5},{5,6},{6,7},{8,9},{9,10},{10,11},{12,13},{... | collective-permute-start | bytes 3080 | tf_op jit(solution)/shard_map/ppermute | solution.py:18
  118.5 6.7 %collective-permute-start.12 = (f32[1,16,128]{2,0,1:T(1,128)S(1)}, f32[1,16,128]{2,0,1:T(1,128)S(1)}, u32[]{:S(2)}, u32[]{:S(2)}) collective-permute-start(f32[1,16,128]{2,0,1:T(1,128)S(1)} %slice.211), channel_id=1, source_target_pairs={{16,0},{17,1},{18,2},{19,3},{20,4},{21,5},{22,6},{23,7},{24,8},{25... | collective-permute-start | bytes 24584 | tf_op jit(solution)/shard_map/ppermute | solution.py:18
  119.8 5.5 %collective-permute-start.13 = (f32[16,1,128]{2,0,1:T(8,128)S(1)}, f32[16,1,128]{2,0,1:T(8,128)S(1)}, u32[]{:S(2)}, u32[]{:S(2)}) collective-permute-start(f32[16,1,128]{2,0,1:T(8,128)S(1)} %slice.213), channel_id=1, source_target_pairs={{4,0},{8,4},{12,8},{5,1},{9,5},{13,9},{6,2},{10,6},{14,10},{7,3},{... | collective-permute-start | bytes 24584 | tf_op jit(solution)/shard_map/ppermute | solution.py:18
  121.1 4.1 %collective-permute-start.14 = (f32[16,16,1]{2,0,1:T(8,128)S(1)}, f32[16,16,1]{2,0,1:T(8,128)S(1)}, u32[]{:S(2)}, u32[]{:S(2)}) collective-permute-start(f32[16,16,1]{2,0,1:T(8,128)S(1)} %bitcast.154), channel_id=1, source_target_pairs={{1,0},{2,1},{3,2},{5,4},{6,5},{7,6},{9,8},{10,9},{11,10},{13,12},{... | collective-permute-start | bytes 3080 | tf_op jit(solution)/shard_map/ppermute | solution.py:18
  125.9 15.9 %collective-permute-start.15 = (f32[1,16,128]{2,0,1:T(1,128)S(1)}, f32[1,16,128]{2,0,1:T(1,128)S(1)}, u32[]{:S(2)}, u32[]{:S(2)}) collective-permute-start(f32[1,16,128]{2,0,1:T(1,128)S(1)} %slice_bitcast_fusion.19), channel_id=1, source_target_pairs={{0,16},{1,17},{2,18},{3,19},{4,20},{5,21},{6,22},{7,23},{8,24},{9,... | collective-permute-start | bytes 24584 | tf_op jit(solution)/shard_map/ppermute | solution.py:18
  130.5 11.4 %collective-permute-start.16 = (f32[16,1,128]{2,0,1:T(8,128)S(1)}, f32[16,1,128]{2,0,1:T(8,128)S(1)}, u32[]{:S(2)}, u32[]{:S(2)}) collective-permute-start(f32[16,1,128]{2,0,1:T(8,128)S(1)} %slice_bitcast_fusion.18), channel_id=1, source_target_pairs={{0,4},{4,8},{8,12},{1,5},{5,9},{9,13},{2,6},{6,10},{10,14},{3,7},{... | collective-permute-start | bytes 24584 | tf_op jit(solution)/shard_map/ppermute | solution.py:18
  134.8 7.1 %collective-permute-start.17 = (f32[16,16,1]{2,0,1:T(8,128)S(1)}, f32[16,16,1]{2,0,1:T(8,128)S(1)}, u32[]{:S(2)}, u32[]{:S(2)}) collective-permute-start(f32[16,16,1]{2,0,1:T(8,128)S(1)} %copy.30), channel_id=1, source_target_pairs={{0,1},{1,2},{2,3},{4,5},{5,6},{6,7},{8,9},{9,10},{10,11},{12,13},{... | collective-permute-start | bytes 3080 | tf_op jit(solution)/shard_map/ppermute | solution.py:18
Sparse Core Ops, SparseCore 0:
  15.6 14.4 reduce-scatter.1
where the time goes:
time: 151 us; the launch traced here: 150 us
  starting transfers between devices  54.2 us (36%)
  blocking collectives  39.5 us (26%)
  waiting for transfers between devices  25.2 us (17%)
  between operations  15.3 us (10%)
  matrix products  7.36 us (5%)
  local copies, waits for them, and re-layouts  4.11 us (3%)
  other arithmetic  3.94 us (3%)
    ppermute x18, starting transfers between devices, from_behind(): return lax.ppermute(block, axis, route)  54.2 us
    psum x1, blocking collectives, shards(): square_sum = lax.psum(jnp.sum(gradient * gradient), ('gx', 'gy', 'gz'))  39.5 us
    reduce_scatter x1, waiting for transfers between devices, shards(): lax.psum_scatter(jnp.einsum('gx,gxyz->xyz', own_signs, partials, precisio...  14.6 us
    ppermute x18, waiting for transfers between devices, from_behind(): return lax.ppermute(block, axis, route)  10.5 us
    dot_general x1, matrix products, shards(): jnp.einsum('gx,gxyz->xyz', own_signs, partials, precision=lax.Precision.H...  6.44 us
  transfers between devices with their start and end apart: 19, of which 10 were waited for; matrix products, arithmetic and copies ran while one was open for 1% of the time, Pallas kernels for 0%

commit v1 on v0

v1 whole, which is shorter than its diff:
```python
import functools

import jax
import jax.numpy as jnp
from jax import lax
from jax.experimental import pallas as pl
from jax.experimental.pallas import tpu as pltpu
from jax.sharding import PartitionSpec as P

ITERS = 3
H = ITERS
SEG = 16
PIECES = 2

step_length = 0.5
tv_weight = 0.2
dual_step = 0.28
primal_step = 0.28
MESH = pl.DeviceIdType.MESH


def kernel(
    dims,
    partials,
    code_bits,
    group_map,
    velocity,
    gradient_out,
    model_out,
    bits,
    gmap,
    part,
    psum,
    vw,
    gw,
    xr,
    xh,
    ys,
    yr,
    ss,
    zr,
    ds,
    dr,
    za,
    va,
    ga,
    target,
    current,
    extra,
    dx,
    dy,
    dz,
    ar,
    result,
    in_sem,
    part_sem,
    xs_sem,
    xr_sem,
    xhs_sem,
    xhr_sem,
    vs_sem,
    vr_sem,
    hs_sem,
    hr_sem,
    ars_sem,
    arr_sem,
    out_sem,
    chain_sem,
):
    nx, ny, nz, slots, bx, by, bz = dims
    rows_all = nx * bx
    sides = min(2, nx - 1)
    win = bx + H * sides
    groups = bz // SEG
    tiles = -(-win // groups)
    yp = -(-(by + 2 * H) // 8) * 8
    ix, iy, iz = lax.axis_index("gx"), lax.axis_index("gy"), lax.axis_index("gz")

    def offset(q):
        return jnp.where(q == 0, 0, jnp.where(q == nx - 1, win - bx, H)) if nx > 1 else 0

    off = offset(ix)
    size = bx // PIECES
    order = [(d, p) for d in list(range(1, nx)) + [0] for p in range(PIECES)]

    def first_row(d, p):
        return lax.rem(ix + d, nx) * bx + p * size

    in_copies = [
        pltpu.make_async_copy(code_bits, bits, in_sem.at[0]),
        pltpu.make_async_copy(group_map, gmap, in_sem.at[1]),
    ]
    v_copy = pltpu.make_async_copy(velocity, vw.at[pl.ds(off, bx)], in_sem.at[2])
    for c in in_copies:
        c.start()
    part_copies = []
    for n, (d, p) in enumerate(order):
        where = pl.ds(first_row(d, p), size)
        part_copies.append(
            pltpu.make_async_copy(partials.at[:, where], part.at[:, where], part_sem.at[n])
        )
    for c in part_copies:
        c.start()
    v_copy.start()

    barrier = pltpu.get_barrier_semaphore()

    def at(x=None, y=None, z=None):
        return (ix if x is None else x, iy if y is None else y, iz if z is None else z)

    def notify(sem, device):
        pl.semaphore_signal(sem, inc=1, device_id=device, device_id_type=MESH)

    for buffer in (yr, zr, dr, va, ga, za, xh, dx, dy, dz, extra, target, current):
        buffer[...] = jnp.zeros_like(buffer)

    if nx > 1:
        @pl.when(ix > 0)
        def _():
            for r in range(H):
                vw[off - H + r] = jnp.zeros((by, bz), jnp.float32)

        @pl.when(ix < nx - 1)
        def _():
            for r in range(H):
                vw[off + bx + r] = jnp.zeros((by, bz), jnp.float32)

    for d in range(1, nx):
        notify(barrier, at(x=lax.rem(ix + d, nx)))
    has = {
        "y-": iy > 0,
        "y+": iy < ny - 1,
        "z-": iz > 0,
        "z+": iz < nz - 1,
    }
    near = {
        "y-": at(y=iy - 1),
        "y+": at(y=iy + 1),
        "z-": at(z=iz - 1),
        "z+": at(z=iz + 1),
    }
    total = jnp.int32(nx - 1)
    for key in has:
        total = total + has[key].astype(jnp.int32)

        @pl.when(has[key])
        def _(key=key):
            notify(barrier, near[key])

    for c in in_copies:
        c.wait()
    pl.semaphore_wait(barrier, total)

    codes = [gmap[ix * slots + s] for s in range(slots)]

    def reduce_rows(first):
        def one(r, carry):
            row = first + r
            acc = None
            for s in range(slots):
                sign = (2 * bits[codes[s], row] - 1).astype(jnp.float32)
                term = sign * part[s, row]
                acc = term if acc is None else acc + term
            psum[row] = acc
            return carry

        lax.fori_loop(0, size, one, 0, unroll=2)

    def x_copy(d, p):
        return pltpu.make_async_remote_copy(
            src_ref=psum.at[pl.ds(first_row(d, p), size)],
            dst_ref=xr.at[d - 1, pl.ds(p * size, size)],
            send_sem=xs_sem.at[d - 1, p],
            recv_sem=xr_sem.at[d - 1, p],
            device_id=at(x=lax.rem(ix + d, nx)),
            device_id_type=MESH,
        )

    for n, (d, p) in enumerate(order):
        part_copies[n].wait()
        reduce_rows(first_row(d, p))
        if d > 0:
            x_copy(d, p).start()

    def halo_copy(d, side):
        q = lax.rem(ix + d, nx)
        first = q * bx - H if side == 0 else q * bx + bx
        return pltpu.make_async_remote_copy(
            src_ref=psum.at[pl.ds(first, H)],
            dst_ref=xh.at[d - 1, side],
            send_sem=xhs_sem.at[d - 1, side],
            recv_sem=xhr_sem.at[d - 1, side],
            device_id=at(x=q),
            device_id_type=MESH,
        )

    def v_halo(side):
        q = ix + 1 if side == 0 else ix - 1
        src = off + bx - H if side == 0 else off
        dst = offset(q) - H if side == 0 else offset(q) + bx
        return pltpu.make_async_remote_copy(
            src_ref=vw.at[pl.ds(src, H)],
            dst_ref=vw.at[pl.ds(dst, H)],
            send_sem=vs_sem.at[side],
            recv_sem=vr_sem.at[side],
            device_id=at(x=q),
            device_id_type=MESH,
        )

    v_copy.wait()
    for d in range(1, nx):
        q = lax.rem(ix + d, nx)

        @pl.when(q > 0)
        def _(d=d):
            halo_copy(d, 0).start()

        @pl.when(q < nx - 1)
        def _(d=d):
            halo_copy(d, 1).start()

    if nx > 1:
        @pl.when(ix < nx - 1)
        def _():
            v_halo(0).start()

        @pl.when(ix > 0)
        def _():
            v_halo(1).start()

    def chain(up, down, count, index, sems):
        if count == 1:
            return

        @pl.when(index > 0)
        def _():
            pl.semaphore_wait(chain_sem.at[sems], 1)

        @pl.when(index < count - 1)
        def _():
            notify(chain_sem.at[sems], up)
            pl.semaphore_wait(chain_sem.at[sems + 1], 1)

        @pl.when(index > 0)
        def _():
            notify(chain_sem.at[sems + 1], down)

    chain(near["y+"], near["y-"], ny, iy, 0)
    chain(near["z+"], near["z-"], nz, iz, 2)
    for d in range(1, nx):
        notify(chain_sem.at[4], at(x=lax.rem(ix + d, nx)))

    squares = jnp.zeros((by, bz), jnp.float32)
    for p in range(PIECES):
        for d in range(1, nx):
            x_copy(d, p).wait_recv()
        for r in range(p * size, (p + 1) * size):
            row = psum[ix * bx + r]
            for d in range(1, nx):
                row = row + xr[d - 1, r]
            gw[off + r] = row
            squares = squares + row * row
    count = nx * ny * nz
    me = (ix * ny + iy) * nz + iz
    ar[me] = jnp.sum(squares, axis=0, keepdims=True)
    if nx > 1:
        pl.semaphore_wait(chain_sem.at[4], nx - 1)

    def send_square(d, carry):
        other = lax.rem(me + d, count)
        pltpu.make_async_remote_copy(
            src_ref=ar.at[me],
            dst_ref=ar.at[me],
            send_sem=ars_sem,
            recv_sem=arr_sem,
            device_id=(other // (ny * nz), lax.rem(other // nz, ny), lax.rem(other, nz)),
            device_id_type=MESH,
        ).start()
        return carry

    lax.fori_loop(1, count, send_square, 0)
    g_out = pltpu.make_async_copy(gw.at[pl.ds(off, bx)], gradient_out, out_sem.at[0])
    g_out.start()

    for side in range(2):
        if nx == 1:
            break
        present = ix > 0 if side == 0 else ix < nx - 1

        @pl.when(present)
        def _(side=side):
            for d in range(1, nx):
                zone = xh.at[d - 1, side]
                pltpu.make_async_copy(zone, zone, xhr_sem.at[d - 1, side]).wait()
            zone = vw.at[pl.ds(off - H if side == 0 else off + bx, H)]
            pltpu.make_async_copy(zone, zone, vr_sem.at[side]).wait()
            for r in range(H):
                there = ix * bx - H + r if side == 0 else ix * bx + bx + r
                row = psum[there]
                for d in range(1, nx):
                    row = row + xh[d - 1, side, r]
                gw[(off - H if side == 0 else off + bx) + r] = row

    lane = lax.broadcasted_iota(jnp.int32, (1, bz), 1)
    group = lane // SEG
    spot = lax.rem(lane, SEG)

    def roll(value, shift):
        shift = shift % bz
        return value if shift == 0 else pltpu.roll(value, shift, 1)

    def pack(read, k):
        acc = None
        for g in range(groups):
            x = tiles * g + k
            if x >= win:
                continue
            moved = roll(read(x), H + SEG * g)
            acc = moved if acc is None else jnp.where(group == g, moved, acc)
        return acc

    fields = (vw, gw)
    for f, field in enumerate(fields):
        for x in range(win):
            tile = field[x]
            ys[0, f, x * H : x * H + H] = tile[by - H : by]
            ys[1, f, x * H : x * H + H] = tile[0:H]
        for k in range(tiles):
            tile = pack(lambda x: field[x], k)
            ss[f, k] = tile
            ds[0, f, k * H : k * H + H] = tile[by - H : by]
            ds[1, f, k * H : k * H + H] = tile[0:H]

    def send(src, dst, n, device):
        return pltpu.make_async_remote_copy(
            src_ref=src,
            dst_ref=dst,
            send_sem=hs_sem.at[n],
            recv_sem=hr_sem.at[n],
            device_id=device,
            device_id_type=MESH,
        )

    both = lambda a, b: jnp.logical_and(has[a], has[b])
    exchange = [
        (send(ys.at[0], yr.at[0], 0, near["y+"]), has["y+"], has["y-"]),
        (send(ys.at[1], yr.at[1], 1, near["y-"]), has["y-"], has["y+"]),
        (send(ss, zr.at[0], 2, near["z+"]), has["z+"], has["z-"]),
        (send(ss, zr.at[1], 3, near["z-"]), has["z-"], has["z+"]),
        (send(ds.at[0], dr.at[0], 4, at(y=iy + 1, z=iz + 1)), both("y+", "z+"), both("y-", "z-")),
        (send(ds.at[0], dr.at[1], 5, at(y=iy + 1, z=iz - 1)), both("y+", "z-"), both("y-", "z+")),
        (send(ds.at[1], dr.at[2], 6, at(y=iy - 1, z=iz + 1)), both("y-", "z+"), both("y+", "z-")),
        (send(ds.at[1], dr.at[3], 7, at(y=iy - 1, z=iz - 1)), both("y-", "z-"), both("y+", "z+")),
    ]
    for copy, sends, _ in exchange:
        pl.when(sends)(copy.start)
    for copy, _, receives in exchange:
        pl.when(receives)(copy.wait_recv)

    front = 8

    def base(x):
        return front + x * yp

    for f, (field, whole) in enumerate(((vw, va), (gw, ga))):
        for x in range(win):
            b = base(x)
            whole[b + H : b + H + by] = field[x]
            whole[b : b + H] = yr[0, f, x * H : x * H + H]
            whole[b + H + by : b + 2 * H + by] = yr[1, f, x * H : x * H + H]
        for k in range(tiles):
            for z in range(2):
                za[z, H : H + by] = zr[z, f, k]
                za[z, 0:H] = dr[z, f, k * H : k * H + H]
                za[z, H + by : 2 * H + by] = dr[2 + z, f, k * H : k * H + H]
            left = za[0, 0:yp]
            mine = pack(lambda x: whole[base(x) : base(x) + yp], k)
            right = roll(za[1, 0:yp], SEG // 2)
            b = base(win + k)
            whole[b : b + yp] = jnp.where(
                spot < H,
                left,
                jnp.where(
                    spot < SEG // 2,
                    mine,
                    jnp.where(spot < SEG // 2 + H, roll(mine, SEG // 2), right),
                ),
            )

    many = ar.at[pl.ds(0, count - 1)]
    pltpu.make_async_copy(many, many, arr_sem).wait()
    square_sum = jnp.sum(jnp.sum(ar[...], axis=0), axis=1, keepdims=True)
    cells = nx * ny * nz * bx * by * bz
    scale = step_length * lax.rsqrt(square_sum / cells + 1.0)

    y_at = iy * by - H + lax.broadcasted_iota(jnp.int32, (yp, 1), 0)
    keep_y = jnp.logical_and(y_at >= 0, y_at < ny * by - 1)
    keep_y = jnp.broadcast_to(keep_y, (yp, bz))
    z_main = iz * bz + lane
    keep_z_main = jnp.broadcast_to(z_main < nz * bz - 1, (yp, bz))
    z_pack = iz * bz + jnp.where(spot < SEG // 2, spot - H, spot - SEG // 2 + bz - H)
    keep_z_pack = jnp.broadcast_to(
        jnp.logical_and(z_pack >= 0, z_pack < nz * bz - 1), (yp, bz)
    )
    start = ix * bx - off
    blocks = win + tiles

    def rows(ref, x, shift=0):
        return ref[base(x) + shift : base(x) + shift + yp]

    for x in range(blocks):
        value = rows(va, x) - scale * rows(ga, x)
        target[base(x) : base(x) + yp] = value

    for it in range(ITERS):
        now = target if it == 0 else extra
        held = target if it == 0 else current
        last = it == ITERS - 1
        for x in range(blocks):
            here = rows(now, x)
            b = base(x)
            ddy = jnp.where(keep_y, rows(now, x, 1) - here, 0.0)
            if x < win:
                g, k = x // tiles, x % tiles
                edge = roll(rows(now, win + k), bz - 1 - (SEG * g + SEG // 2 + H))
                after = jnp.where(lane == bz - 1, edge, roll(here, -1))
                ddz = jnp.where(keep_z_main, after - here, 0.0)
                if x == win - 1:
                    ddx = jnp.zeros_like(here)
                else:
                    ddx = rows(now, x + 1) - here
            else:
                k = x - win
                ddz = jnp.where(keep_z_pack, roll(here, -1) - here, 0.0)
                if k < tiles - 1:
                    after = rows(now, x + 1)
                else:
                    after = roll(rows(now, win), -SEG)
                ddx = jnp.where(tiles * group + k < win - 1, after - here, 0.0)
            px, py, pz = dual_step * ddx, dual_step * ddy, dual_step * ddz
            if it > 0:
                px, py, pz = rows(dx, x) + px, rows(dy, x) + py, rows(dz, x) + pz
            shrink = jnp.minimum(1.0, tv_weight * lax.rsqrt(px * px + py * py + pz * pz))
            dx[b : b + yp] = px * shrink
            dy[b : b + yp] = py * shrink
            dz[b : b + yp] = pz * shrink
        for x in range(win if last else blocks):
            b = base(x)
            qx, qy, qz = rows(dx, x), rows(dy, x), rows(dz, x)
            spread = qy - rows(dy, x, -1)
            if x < win:
                g, k = x // tiles, x % tiles
                edge = roll(rows(dz, win + k), -(SEG * g + H - 1))
                spread = spread + (qz - jnp.where(lane == 0, edge, roll(qz, 1)))
                spread = spread + (qx if x == 0 else qx - rows(dx, x - 1))
            else:
                k = x - win
                spread = spread + (qz - roll(qz, 1))
                before = rows(dx, x - 1) if k > 0 else roll(rows(dx, blocks - 1), SEG)
                spread = spread + (qx - before)
            old = rows(held, x)
            new = (old + primal_step * (spread + rows(target, x))) * (1.0 / (1.0 + primal_step))
            if last:
                result[x] = new[H : H + by]
            else:
                current[b : b + yp] = new
                extra[b : b + yp] = 2.0 * new - old

    m_out = pltpu.make_async_copy(result.at[pl.ds(off, bx)], model_out, out_sem.at[1])
    m_out.start()

    for d in range(1, nx):
        for p in range(PIECES):
            x_copy(d, p).wait_send()
        q = lax.rem(ix + d, nx)
        pl.when(q > 0)(halo_copy(d, 0).wait_send)
        pl.when(q < nx - 1)(halo_copy(d, 1).wait_send)
    if nx > 1:
        pl.when(ix < nx - 1)(v_halo(0).wait_send)
        pl.when(ix > 0)(v_halo(1).wait_send)
    for copy, sends, _ in exchange:
        pl.when(sends)(copy.wait_send)
    pltpu.make_async_copy(many, many, ars_sem).wait()
    g_out.wait()
    m_out.wait()


def shards(partials, code_bits, group_map, velocity):
    slots = partials.shape[0]
    bx, by, bz = velocity.shape
    nx, ny, nz = (lax.axis_size(a) for a in ("gx", "gy", "gz"))
    dims = (nx, ny, nz, slots, bx, by, bz)
    win = bx + H * min(2, nx - 1)
    tiles = -(-win // (bz // SEG))
    yp = -(-(by + 2 * H) // 8) * 8
    flat = 16 + (win + tiles) * yp
    strip = -(-(win * H + 5) // 8) * 8
    diag = -(-(tiles * H + 5) // 8) * 8
    f32 = functools.partial(pltpu.VMEM, dtype=jnp.float32)
    peers = max(nx - 1, 1)
    dma = pltpu.SemaphoreType.DMA
    anywhere = pl.BlockSpec(memory_space=pl.ANY)
    block = jax.ShapeDtypeStruct(velocity.shape, jnp.float32)
    return pl.pallas_call(
        functools.partial(kernel, dims),
        out_shape=(block, block),
        in_specs=[anywhere] * 4,
        out_specs=(anywhere, anywhere),
        scratch_shapes=[
            pltpu.SMEM(code_bits.shape, jnp.int32),
            pltpu.SMEM(group_map.shape, jnp.int32),
            f32(partials.shape),
            f32((nx * bx, by, bz)),
            f32((win, by, bz)),
            f32((win, by, bz)),
            f32((peers, bx, by, bz)),
            f32((peers, 2, H, by, bz)),
            f32((2, 2, strip, bz)),
            f32((2, 2, strip, bz)),
            f32((2, tiles, by, bz)),
            f32((2, 2, tiles, by, bz)),
            f32((2, 2, diag, bz)),
            f32((4, 2, diag, bz)),
            f32((2, yp + 8, bz)),
        ]
        + [f32((flat, bz))] * 8
        + [
            f32((nx * ny * nz, 1, bz)),
            f32((win, by, bz)),
            dma((3,)),
            dma((nx * PIECES,)),
            dma((peers, PIECES)),
            dma((peers, PIECES)),
            dma((peers, 2)),
            dma((peers, 2)),
            dma((2,)),
            dma((2,)),
            dma((8,)),
            dma((8,)),
            dma,
            dma,
            dma((2,)),
            pltpu.SemaphoreType.REGULAR((5,)),
        ],
        compiler_params=pltpu.CompilerParams(collective_id=0, has_side_effects=True),
    )(partials, code_bits, group_map, velocity)


def solution(mesh):
    placed = (P("gx", None, "gy", "gz"), P(), P(), P("gx", "gy", "gz"))
    return jax.shard_map(
        shards,
        mesh=mesh,
        in_specs=placed,
        out_specs=(P("gx", "gy", "gz"), P("gx", "gy", "gz")),
        check_vma=False,
    )
```

time: 151 us -> 24.4 us (0.16)
  starting transfers between devices: 54.2 us -> 0 us
  blocking collectives: 39.5 us -> 0 us
  waiting for transfers between devices: 25.2 us -> 0 us
  Pallas kernels: 0 us -> 20.5 us
  between operations: 15.3 us -> 0.64 us
  matrix products: 7.36 us -> 0 us
  other arithmetic: 3.94 us -> 0 us
    ppermute x18 -> x0, starting transfers between devices: 54.2 us -> none  [from_behind(): return lax.ppermute(block, axis, route)]
    psum x1 -> x0, blocking collectives: 39.5 us -> none  [shards(): square_sum = lax.psum(jnp.sum(gradient * gradient), ('gx', 'gy', 'gz'))]
    pallas_call x0 -> x1, Pallas kernels: none -> 20.5 us  [shards(): pl.pallas_call(functools.partial(kernel, dims), out_shape=(block, block),...]
    reduce_scatter x1 -> x0, waiting for transfers between devices: 14.6 us -> none  [shards(): lax.psum_scatter(jnp.einsum('gx,gxyz->xyz', own_signs, partials, precisio...]
    ppermute x18 -> x0, waiting for transfers between devices: 10.5 us -> none  [from_behind(): return lax.ppermute(block, axis, route)]
    dot_general x2 -> x0, matrix products: 7.36 us -> none  [the longest x1 6.44 us: shards(): jnp.einsum('gx,gxyz->xyz', own_signs, partials, precision=lax.Precision.H...]
    reduce_sum x4 -> x0, other arithmetic: 1.81 us -> none  [the longest x1 1.54 us: shards(): square_sum = lax.psum(jnp.sum(gradient * gradient), ('gx', 'gy', 'gz'))]
    unnamed x6 -> x2, local copies, waits for them, and re-layouts: 1.4 us -> 3.14 us
  transfers between devices with their start and end apart: 19 -> 0, of which waited for: 10 -> 0; matrix products, arithmetic and copies ran while one was open for 1% -> 0% of each run, Pallas kernels for 0% -> 0%
where the time goes in v1:
time: 24.4 us; the launch traced here: 24.2 us
  Pallas kernels  20.5 us (84%)
  local copies, waits for them, and re-layouts  3.14 us (13%)
  between operations  0.64 us (3%)
    pallas_call x1, Pallas kernels, shards(): pl.pallas_call(functools.partial(kernel, dims), out_shape=(block, block),...  20.5 us
    unnamed x2, local copies, waits for them, and re-layouts  3.14 us

profile of v1, /device:TPU:0, one launch (start us, length us, event | category | flops | bytes accessed | tf_op | source)
XLA Modules:
  0.0 24.2 jit_solution(12433299259199127034)
XLA Ops:
  0.6 20.5 %shard_map.59 = (f32[16,16,128]{2,1,0:T(8,128)}, f32[16,16,128]{2,1,0:T(8,128)}) custom-call(f32[16,32,16,128]{3,2,1,0:T(8,128)} %partials.1, s32[32,32]{1,0:T(8,128)} %code_bits.1, s32[32]{0:T(128)} %group_map.1, f32[16,16,128]{2,1,0:T(8,128)} %velocity.1), custom_call_target="tpu_custom_call" | custom-call | tf_op jit(solution)/shard_map/pallas_call | solution.py:504
  21.1 1.6 %copy.8 = f32[16,16,128]{2,1,0:T(8,128)} copy(f32[16,16,128]{2,1,0:T(8,128)} %get-tuple-element.4) | data formatting | bytes 262144
  22.7 1.6 %copy.9 = f32[16,16,128]{2,1,0:T(8,128)} copy(f32[16,16,128]{2,1,0:T(8,128)} %get-tuple-element.5) | data formatting | bytes 262144

commit v2 on v1

--- a/solution.py
+++ b/solution.py
@@ -10,13 +10,32 @@
 ITERS = 3
 H = ITERS
 SEG = 16
-PIECES = 2
+PIECES = 4
 
 step_length = 0.5
 tv_weight = 0.2
 dual_step = 0.28
 primal_step = 0.28
 MESH = pl.DeviceIdType.MESH
+
+
+def geometry(dims):
+    nx, ny, nz, slots, bx, by, bz = dims
+    win = bx + H * min(2, nx - 1)
+    tiles = -(-win // (bz // SEG))
+    yp = -(-(by + 2 * H) // 8) * 8
+    return win, tiles, yp, 16 + (win + tiles) * yp
+
+
+def own_offset(nx, bx, win, q):
+    if nx == 1:
+        return 0
+    return jnp.where(q == 0, 0, jnp.where(q == nx - 1, win - bx, H))
+
+
+def roll(value, shift):
+    shift = shift % value.shape[1]
+    return value if shift == 0 else pltpu.roll(value, shift, 1)
 
 
 def kernel(
@@ -25,14 +44,15 @@
     code_bits,
     group_map,
     velocity,
-    gradient_out,
-    model_out,
+    va,
+    ga,
+    gw,
+    scale_out,
     bits,
     gmap,
     part,
     psum,
     vw,
-    gw,
     xr,
     xh,
     ys,
@@ -42,16 +62,7 @@
     ds,
     dr,
     za,
-    va,
-    ga,
-    target,
-    current,
-    extra,
-    dx,
-    dy,
-    dz,
     ar,
-    result,
     in_sem,
     part_sem,
     xs_sem,
@@ -64,21 +75,13 @@
     hr_sem,
     ars_sem,
     arr_sem,
-    out_sem,
     chain_sem,
 ):
     nx, ny, nz, slots, bx, by, bz = dims
-    rows_all = nx * bx
-    sides = min(2, nx - 1)
-    win = bx + H * sides
+    win, tiles, yp, flat = geometry(dims)
     groups = bz // SEG
-    tiles = -(-win // groups)
-    yp = -(-(by + 2 * H) // 8) * 8
     ix, iy, iz = lax.axis_index("gx"), lax.axis_index("gy"), lax.axis_index("gz")
-
-    def offset(q):
-        return jnp.where(q == 0, 0, jnp.where(q == nx - 1, win - bx, H)) if nx > 1 else 0
-
+    offset = functools.partial(own_offset, nx, bx, win)
     off = offset(ix)
     size = bx // PIECES
     order = [(d, p) for d in list(range(1, nx)) + [0] for p in range(PIECES)]
@@ -93,6 +96,7 @@
     v_copy = pltpu.make_async_copy(velocity, vw.at[pl.ds(off, bx)], in_sem.at[2])
     for c in in_copies:
         c.start()
+    v_copy.start()
     part_copies = []
     for n, (d, p) in enumerate(order):
         where = pl.ds(first_row(d, p), size)
@@ -101,7 +105,6 @@
         )
     for c in part_copies:
         c.start()
-    v_copy.start()
 
     barrier = pltpu.get_barrier_semaphore()
 
@@ -111,19 +114,8 @@
     def notify(sem, device):
         pl.semaphore_signal(sem, inc=1, device_id=device, device_id_type=MESH)
 
-    for buffer in (yr, zr, dr, va, ga, za, xh, dx, dy, dz, extra, target, current):
+    for buffer in (yr, zr, dr):
         buffer[...] = jnp.zeros_like(buffer)
-
-    if nx > 1:
-        @pl.when(ix > 0)
-        def _():
-            for r in range(H):
-                vw[off - H + r] = jnp.zeros((by, bz), jnp.float32)
-
-        @pl.when(ix < nx - 1)
-        def _():
-            for r in range(H):
-                vw[off + bx + r] = jnp.zeros((by, bz), jnp.float32)
 
     for d in range(1, nx):
         notify(barrier, at(x=lax.rem(ix + d, nx)))
@@ -147,52 +139,9 @@
         def _(key=key):
             notify(barrier, near[key])
 
-    for c in in_copies:
-        c.wait()
+    for buffer in (za, va, ga):
+        buffer[...] = jnp.zeros_like(buffer)
     pl.semaphore_wait(barrier, total)
-
-    codes = [gmap[ix * slots + s] for s in range(slots)]
-
-    def reduce_rows(first):
-        def one(r, carry):
-            row = first + r
-            acc = None
-            for s in range(slots):
-                sign = (2 * bits[codes[s], row] - 1).astype(jnp.float32)
-                term = sign * part[s, row]
-                acc = term if acc is None else acc + term
-            psum[row] = acc
-            return carry
-
-        lax.fori_loop(0, size, one, 0, unroll=2)
-
-    def x_copy(d, p):
-        return pltpu.make_async_remote_copy(
-            src_ref=psum.at[pl.ds(first_row(d, p), size)],
-            dst_ref=xr.at[d - 1, pl.ds(p * size, size)],
-            send_sem=xs_sem.at[d - 1, p],
-            recv_sem=xr_sem.at[d - 1, p],
-            device_id=at(x=lax.rem(ix + d, nx)),
-            device_id_type=MESH,
-        )
-
-    for n, (d, p) in enumerate(order):
-        part_copies[n].wait()
-        reduce_rows(first_row(d, p))
-        if d > 0:
-            x_copy(d, p).start()
-
-    def halo_copy(d, side):
-        q = lax.rem(ix + d, nx)
-        first = q * bx - H if side == 0 else q * bx + bx
-        return pltpu.make_async_remote_copy(
-            src_ref=psum.at[pl.ds(first, H)],
-            dst_ref=xh.at[d - 1, side],
-            send_sem=xhs_sem.at[d - 1, side],
-            recv_sem=xhr_sem.at[d - 1, side],
-            device_id=at(x=q),
-            device_id_type=MESH,
-        )
 
     def v_halo(side):
         q = ix + 1 if side == 0 else ix - 1
@@ -208,17 +157,6 @@
         )
 
     v_copy.wait()
-    for d in range(1, nx):
-        q = lax.rem(ix + d, nx)
-
-        @pl.when(q > 0)
-        def _(d=d):
-            halo_copy(d, 0).start()
-
-        @pl.when(q < nx - 1)
-        def _(d=d):
-            halo_copy(d, 1).start()
-
     if nx > 1:
         @pl.when(ix < nx - 1)
         def _():
@@ -227,6 +165,62 @@
         @pl.when(ix > 0)
         def _():
             v_halo(1).start()
+
+    for c in in_copies:
+        c.wait()
+    codes = [gmap[ix * slots + s] for s in range(slots)]
+
+    def reduce_rows(first):
+        def one(r, carry):
+            row = first + r
+            acc = None
+            for s in range(slots):
+                sign = (2 * bits[codes[s], row] - 1).astype(jnp.float32)
+                term = sign * part[s, row]
+                acc = term if acc is None else acc + term
+            psum[row] = acc
+            return carry
+
+        lax.fori_loop(0, size, one, 0, unroll=2)
+
+    def x_copy(d, p):
+        return pltpu.make_async_remote_copy(
+            src_ref=psum.at[pl.ds(first_row(d, p), size)],
+            dst_ref=xr.at[d - 1, pl.ds(p * size, size)],
+            send_sem=xs_sem.at[d - 1, p],
+            recv_sem=xr_sem.at[d - 1, p],
+            device_id=at(x=lax.rem(ix + d, nx)),
+            device_id_type=MESH,
+        )
+
+    for n, (d, p) in enumerate(order):
+        part_copies[n].wait()
+        reduce_rows(first_row(d, p))
+        if d > 0:
+            x_copy(d, p).start()
+
+    def halo_copy(d, side):
+        q = lax.rem(ix + d, nx)
+        first = q * bx - H if side == 0 else q * bx + bx
+        return pltpu.make_async_remote_copy(
+            src_ref=psum.at[pl.ds(first, H)],
+            dst_ref=xh.at[d - 1, side],
+            send_sem=xhs_sem.at[d - 1, side],
+            recv_sem=xhr_sem.at[d - 1, side],
+            device_id=at(x=q),
+            device_id_type=MESH,
+        )
+
+    for d in range(1, nx):
+        q = lax.rem(ix + d, nx)
+
+        @pl.when(q > 0)
+        def _(d=d):
+            halo_copy(d, 0).start()
+
+        @pl.when(q < nx - 1)
+        def _(d=d):
+            halo_copy(d, 1).start()
 
     def chain(up, down, count, index, sems):
         if count == 1:
@@ -278,9 +272,11 @@
         ).start()
         return carry
 
-    lax.fori_loop(1, count, send_square, 0)
-    g_out = pltpu.make_async_copy(gw.at[pl.ds(off, bx)], gradient_out, out_sem.at[0])
-    g_out.start()
+    if count <= 64:
+        for d in range(count - 1, 0, -1):
+            send_square(d, 0)
+    else:
+        lax.fori_loop(1, count, send_square, 0)
 
     for side in range(2):
         if nx == 1:
@@ -304,10 +300,6 @@
     lane = lax.broadcasted_iota(jnp.int32, (1, bz), 1)
     group = lane // SEG
     spot = lax.rem(lane, SEG)
-
-    def roll(value, shift):
-        shift = shift % bz
-        return value if shift == 0 else pltpu.roll(value, shift, 1)
 
     def pack(read, k):
         acc = None
@@ -393,6 +385,58 @@
     cells = nx * ny * nz * bx * by * bz
     scale = step_length * lax.rsqrt(square_sum / cells + 1.0)
 
+    scale_out[...] = jnp.broadcast_to(scale, scale_out.shape)
+
+    for d in range(1, nx):
+        for p in range(PIECES):
+            x_copy(d, p).wait_send()
+        q = lax.rem(ix + d, nx)
+        pl.when(q > 0)(halo_copy(d, 0).wait_send)
+        pl.when(q < nx - 1)(halo_copy(d, 1).wait_send)
+    if nx > 1:
+        pl.when(ix < nx - 1)(v_halo(0).wait_send)
+        pl.when(ix > 0)(v_halo(1).wait_send)
+    for copy, sends, _ in exchange:
+        pl.when(sends)(copy.wait_send)
+    pltpu.make_async_copy(many, many, ars_sem).wait()
+
+
+def proximal(
+    dims,
+    va,
+    ga,
+    gw,
+    scale_in,
+    gradient_out,
+    model_out,
+    target,
+    current,
+    extra,
+    dx,
+    dy,
+    dz,
+    result,
+    out_sem,
+):
+    nx, ny, nz, slots, bx, by, bz = dims
+    win, tiles, yp, flat = geometry(dims)
+    ix, iy, iz = lax.axis_index("gx"), lax.axis_index("gy"), lax.axis_index("gz")
+    off = own_offset(nx, bx, win, ix)
+    g_out = pltpu.make_async_copy(gw.at[pl.ds(off, bx)], gradient_out, out_sem.at[0])
+    g_out.start()
+    front = 8
+
+    def base(x):
+        return front + x * yp
+
+    edge_rows = jnp.zeros((front, bz), jnp.float32)
+    dy[0:front] = edge_rows
+    target[flat - front : flat] = edge_rows
+    extra[flat - front : flat] = edge_rows
+    scale = scale_in[...]
+    lane = lax.broadcasted_iota(jnp.int32, (1, bz), 1)
+    group = lane // SEG
+    spot = lax.rem(lane, SEG)
     y_at = iy * by - H + lax.broadcasted_iota(jnp.int32, (yp, 1), 0)
     keep_y = jnp.logical_and(y_at >= 0, y_at < ny * by - 1)
     keep_y = jnp.broadcast_to(keep_y, (yp, bz))
@@ -468,19 +512,6 @@
 
     m_out = pltpu.make_async_copy(result.at[pl.ds(off, bx)], model_out, out_sem.at[1])
     m_out.start()
-
-    for d in range(1, nx):
-        for p in range(PIECES):
-            x_copy(d, p).wait_send()
-        q = lax.rem(ix + d, nx)
-        pl.when(q > 0)(halo_copy(d, 0).wait_send)
-        pl.when(q < nx - 1)(halo_copy(d, 1).wait_send)
-    if nx > 1:
-        pl.when(ix < nx - 1)(v_halo(0).wait_send)
-        pl.when(ix > 0)(v_halo(1).wait_send)
-    for copy, sends, _ in exchange:
-        pl.when(sends)(copy.wait_send)
-    pltpu.make_async_copy(many, many, ars_sem).wait()
     g_out.wait()
     m_out.wait()
 
@@ -490,28 +521,26 @@
     bx, by, bz = velocity.shape
     nx, ny, nz = (lax.axis_size(a) for a in ("gx", "gy", "gz"))
     dims = (nx, ny, nz, slots, bx, by, bz)
-    win = bx + H * min(2, nx - 1)
-    tiles = -(-win // (bz // SEG))
-    yp = -(-(by + 2 * H) // 8) * 8
-    flat = 16 + (win + tiles) * yp
+    win, tiles, yp, flat = geometry(dims)
     strip = -(-(win * H + 5) // 8) * 8
     diag = -(-(tiles * H + 5) // 8) * 8
     f32 = functools.partial(pltpu.VMEM, dtype=jnp.float32)
     peers = max(nx - 1, 1)
     dma = pltpu.SemaphoreType.DMA
     anywhere = pl.BlockSpec(memory_space=pl.ANY)
+    near = pl.BlockSpec(memory_space=pltpu.VMEM)
     block = jax.ShapeDtypeStruct(velocity.shape, jnp.float32)
-    return pl.pallas_call(
+    handed = (f32((flat, bz)), f32((flat, bz)), f32((win, by, bz)), f32((1, bz)))
+    assembled = pl.pallas_call(
         functools.partial(kernel, dims),
-        out_shape=(block, block),
-        in_specs=[anywhere] * 4,
-        out_specs=(anywhere, anywhere),
+        out_shape=handed,
+        in_specs=[pl.BlockSpec(memory_space=pltpu.HBM)] * 4,
+        out_specs=(near,) * 4,
         scratch_shapes=[
             pltpu.SMEM(code_bits.shape, jnp.int32),
             pltpu.SMEM(group_map.shape, jnp.int32),
             f32(partials.shape),
             f32((nx * bx, by, bz)),
-            f32((win, by, bz)),
             f32((win, by, bz)),
             f32((peers, bx, by, bz)),
             f32((peers, 2, H, by, bz)),
@@ -522,11 +551,7 @@
             f32((2, 2, diag, bz)),
             f32((4, 2, diag, bz)),
             f32((2, yp + 8, bz)),
-        ]
-        + [f32((flat, bz))] * 8
-        + [
             f32((nx * ny * nz, 1, bz)),
-            f32((win, by, bz)),
             dma((3,)),
             dma((nx * PIECES,)),
             dma((peers, PIECES)),
@@ -539,11 +564,20 @@
             dma((8,)),
             dma,
             dma,
-            dma((2,)),
             pltpu.SemaphoreType.REGULAR((5,)),
         ],
-        compiler_params=pltpu.CompilerParams(collective_id=0, has_side_effects=True),
+        compiler_params=pltpu.CompilerParams(
+            collective_id=0, has_side_effects=True
+        ),
     )(partials, code_bits, group_map, velocity)
+    return pl.pallas_call(
+        functools.partial(proximal, dims),
+        out_shape=(block, block),
+        in_specs=[near] * 4,
+        out_specs=(anywhere, anywhere),
+        scratch_shapes=[f32((flat, bz))] * 6 + [f32((win, by, bz)), dma((2,))],
+        compiler_params=pltpu.CompilerParams(vmem_limit_bytes=32 * 2**20),
+    )(*assembled)
 
 
 def solution(mesh):

time: 24.4 us -> 21.6 us (0.89)
  local copies, waits for them, and re-layouts: 3.14 us -> 0 us
  Pallas kernels: 20.5 us -> 20.8 us
    unnamed x2 -> x0, local copies, waits for them, and re-layouts: 3.14 us -> none
    pallas_call x1 -> x2, Pallas kernels: 20.5 us -> 20.8 us  [the longest x1 18.8 us: shards(): pl.pallas_call(functools.partial(kernel, dims), out_shape=handed, in_spec...]
where the time goes in v2:
time: 21.6 us; the launch traced here: 21.4 us
  Pallas kernels  20.8 us (96%)
  between operations  0.64 us (3%)
    pallas_call x1, Pallas kernels, shards(): pl.pallas_call(functools.partial(kernel, dims), out_shape=handed, in_spec...  18.8 us
    pallas_call x1, Pallas kernels, shards(): pl.pallas_call(functools.partial(proximal, dims), out_shape=(block, block...  1.94 us

profile of v2, /device:TPU:0, one launch (start us, length us, event | category | flops | bytes accessed | tf_op | source)
XLA Modules:
  0.0 21.4 jit_solution(8389066735477611418)
XLA Ops:
  0.6 18.8 %shard_map.59 = (f32[544,128]{1,0:T(8,128)S(1)}, f32[544,128]{1,0:T(8,128)S(1)}, f32[19,16,128]{2,1,0:T(8,128)S(1)}, f32[1,128]{1,0:T(1,128)S(1)}) custom-call(f32[16,32,16,128]{3,2,1,0:T(8,128)} %partials.1, s32[32,32]{1,0:T(8,128)} %code_bits.1, s32[32]{0:T(128)} %group_map.1, f32[16,16,128]{2,1,0:T(8,128)} %velocity.1), custom_call_target="tpu_custom_call" | custom-call | tf_op jit(solution)/shard_map/pallas_call | solution.py:534
  19.5 1.9 %shard_map.60 = (f32[16,16,128]{2,1,0:T(8,128)}, f32[16,16,128]{2,1,0:T(8,128)}) custom-call(f32[544,128]{1,0:T(8,128)S(1)} %get-tuple-element.6.va, f32[544,128]{1,0:T(8,128)S(1)} %get-tuple-element.7.ga, f32[19,16,128]{2,1,0:T(8,128)S(1)} %get-tuple-element.8.gw, f32[1,128]{1,0:T(1,128)S(1)} %get-tuple-element.9.scale_in), custom_call_target="tpu_custom_call" | custom-call | tf_op jit(solution)/shard_map/pallas_call | solution.py:573

commit v3 on v2

--- a/solution.py
+++ b/solution.py
@@ -244,59 +244,6 @@
     for d in range(1, nx):
         notify(chain_sem.at[4], at(x=lax.rem(ix + d, nx)))
 
-    squares = jnp.zeros((by, bz), jnp.float32)
-    for p in range(PIECES):
-        for d in range(1, nx):
-            x_copy(d, p).wait_recv()
-        for r in range(p * size, (p + 1) * size):
-            row = psum[ix * bx + r]
-            for d in range(1, nx):
-                row = row + xr[d - 1, r]
-            gw[off + r] = row
-            squares = squares + row * row
-    count = nx * ny * nz
-    me = (ix * ny + iy) * nz + iz
-    ar[me] = jnp.sum(squares, axis=0, keepdims=True)
-    if nx > 1:
-        pl.semaphore_wait(chain_sem.at[4], nx - 1)
-
-    def send_square(d, carry):
-        other = lax.rem(me + d, count)
-        pltpu.make_async_remote_copy(
-            src_ref=ar.at[me],
-            dst_ref=ar.at[me],
-            send_sem=ars_sem,
-            recv_sem=arr_sem,
-            device_id=(other // (ny * nz), lax.rem(other // nz, ny), lax.rem(other, nz)),
-            device_id_type=MESH,
-        ).start()
-        return carry
-
-    if count <= 64:
-        for d in range(count - 1, 0, -1):
-            send_square(d, 0)
-    else:
-        lax.fori_loop(1, count, send_square, 0)
-
-    for side in range(2):
-        if nx == 1:
-            break
-        present = ix > 0 if side == 0 else ix < nx - 1
-
-        @pl.when(present)
-        def _(side=side):
-            for d in range(1, nx):
-                zone = xh.at[d - 1, side]
-                pltpu.make_async_copy(zone, zone, xhr_sem.at[d - 1, side]).wait()
-            zone = vw.at[pl.ds(off - H if side == 0 else off + bx, H)]
-            pltpu.make_async_copy(zone, zone, vr_sem.at[side]).wait()
-            for r in range(H):
-                there = ix * bx - H + r if side == 0 else ix * bx + bx + r
-                row = psum[there]
-                for d in range(1, nx):
-                    row = row + xh[d - 1, side, r]
-                gw[(off - H if side == 0 else off + bx) + r] = row
-
     lane = lax.broadcasted_iota(jnp.int32, (1, bz), 1)
     group = lane // SEG
     spot = lax.rem(lane, SEG)
@@ -311,8 +258,7 @@
             acc = moved if acc is None else jnp.where(group == g, moved, acc)
         return acc
 
-    fields = (vw, gw)
-    for f, field in enumerate(fields):
+    def prepare(f, field):
         for x in range(win):
             tile = field[x]
             ys[0, f, x * H : x * H + H] = tile[by - H : by]
@@ -323,38 +269,47 @@
             ds[0, f, k * H : k * H + H] = tile[by - H : by]
             ds[1, f, k * H : k * H + H] = tile[0:H]
 
-    def send(src, dst, n, device):
-        return pltpu.make_async_remote_copy(
-            src_ref=src,
-            dst_ref=dst,
-            send_sem=hs_sem.at[n],
-            recv_sem=hr_sem.at[n],
-            device_id=device,
-            device_id_type=MESH,
-        )
-
     both = lambda a, b: jnp.logical_and(has[a], has[b])
-    exchange = [
-        (send(ys.at[0], yr.at[0], 0, near["y+"]), has["y+"], has["y-"]),
-        (send(ys.at[1], yr.at[1], 1, near["y-"]), has["y-"], has["y+"]),
-        (send(ss, zr.at[0], 2, near["z+"]), has["z+"], has["z-"]),
-        (send(ss, zr.at[1], 3, near["z-"]), has["z-"], has["z+"]),
-        (send(ds.at[0], dr.at[0], 4, at(y=iy + 1, z=iz + 1)), both("y+", "z+"), both("y-", "z-")),
-        (send(ds.at[0], dr.at[1], 5, at(y=iy + 1, z=iz - 1)), both("y+", "z-"), both("y-", "z+")),
-        (send(ds.at[1], dr.at[2], 6, at(y=iy - 1, z=iz + 1)), both("y-", "z+"), both("y+", "z-")),
-        (send(ds.at[1], dr.at[3], 7, at(y=iy - 1, z=iz - 1)), both("y-", "z-"), both("y+", "z+")),
-    ]
-    for copy, sends, _ in exchange:
-        pl.when(sends)(copy.start)
-    for copy, _, receives in exchange:
-        pl.when(receives)(copy.wait_recv)
+
+    def exchange(f):
+        def send(src, dst, n, device):
+            return pltpu.make_async_remote_copy(
+                src_ref=src.at[f],
+                dst_ref=dst.at[f],
+                send_sem=hs_sem.at[f, n],
+                recv_sem=hr_sem.at[f, n],
+                device_id=device,
+                device_id_type=MESH,
+            )
+
+        up, down = ds.at[0], ds.at[1]
+        pp, pm = both("y+", "z+"), both("y+", "z-")
+        mp, mm = both("y-", "z+"), both("y-", "z-")
+        return [
+            (send(ys.at[0], yr.at[0], 0, near["y+"]), has["y+"], has["y-"]),
+            (send(ys.at[1], yr.at[1], 1, near["y-"]), has["y-"], has["y+"]),
+            (send(ss, zr.at[0], 2, near["z+"]), has["z+"], has["z-"]),
+            (send(ss, zr.at[1], 3, near["z-"]), has["z-"], has["z+"]),
+            (send(up, dr.at[0], 4, at(y=iy + 1, z=iz + 1)), pp, mm),
+            (send(up, dr.at[1], 5, at(y=iy + 1, z=iz - 1)), pm, mp),
+            (send(down, dr.at[2], 6, at(y=iy - 1, z=iz + 1)), mp, pm),
+            (send(down, dr.at[3], 7, at(y=iy - 1, z=iz - 1)), mm, pp),
+        ]
+
+    def send_all(f):
+        for copy, sends, _ in exchange(f):
+            pl.when(sends)(copy.start)
+
+    def receive_all(f):
+        for copy, _, receives in exchange(f):
+            pl.when(receives)(copy.wait_recv)
 
     front = 8
 
     def base(x):
         return front + x * yp
 
-    for f, (field, whole) in enumerate(((vw, va), (gw, ga))):
+    def assemble(f, field, whole):
         for x in range(win):
             b = base(x)
             whole[b + H : b + H + by] = field[x]
@@ -379,6 +334,72 @@
                 ),
             )
 
+    if nx > 1:
+        for side in range(2):
+            zone = vw.at[pl.ds(off - H if side == 0 else off + bx, H)]
+            arrived = pltpu.make_async_copy(zone, zone, vr_sem.at[side])
+            pl.when(ix > 0 if side == 0 else ix < nx - 1)(arrived.wait)
+    prepare(0, vw)
+    send_all(0)
+
+    squares = jnp.zeros((by, bz), jnp.float32)
+    for p in range(PIECES):
+        for d in range(1, nx):
+            x_copy(d, p).wait_recv()
+        for r in range(p * size, (p + 1) * size):
+            row = psum[ix * bx + r]
+            for d in range(1, nx):
+                row = row + xr[d - 1, r]
+            gw[off + r] = row
+            squares = squares + row * row
+    count = nx * ny * nz
+    me = (ix * ny + iy) * nz + iz
+    ar[me] = jnp.sum(squares, axis=0, keepdims=True)
+    if nx > 1:
+        pl.semaphore_wait(chain_sem.at[4], nx - 1)
+
+    def send_square(d, carry):
+        other = lax.rem(me + d, count)
+        pltpu.make_async_remote_copy(
+            src_ref=ar.at[me],
+            dst_ref=ar.at[me],
+            send_sem=ars_sem,
+            recv_sem=arr_sem,
+            device_id=(other // (ny * nz), lax.rem(other // nz, ny), lax.rem(other, nz)),
+            device_id_type=MESH,
+        ).start()
+        return carry
+
+    if count <= 64:
+        for d in range(count - 1, 0, -1):
+            send_square(d, 0)
+    else:
+        lax.fori_loop(1, count, send_square, 0)
+
+    for side in range(2):
+        if nx == 1:
+            break
+        present = ix > 0 if side == 0 else ix < nx - 1
+
+        @pl.when(present)
+        def _(side=side):
+            for d in range(1, nx):
+                zone = xh.at[d - 1, side]
+                pltpu.make_async_copy(zone, zone, xhr_sem.at[d - 1, side]).wait()
+            for r in range(H):
+                there = ix * bx - H + r if side == 0 else ix * bx + bx + r
+                row = psum[there]
+                for d in range(1, nx):
+                    row = row + xh[d - 1, side, r]
+                gw[(off - H if side == 0 else off + bx) + r] = row
+
+    prepare(1, gw)
+    send_all(1)
+    receive_all(0)
+    assemble(0, vw, va)
+    receive_all(1)
+    assemble(1, gw, ga)
+
     many = ar.at[pl.ds(0, count - 1)]
     pltpu.make_async_copy(many, many, arr_sem).wait()
     square_sum = jnp.sum(jnp.sum(ar[...], axis=0), axis=1, keepdims=True)
@@ -396,8 +417,9 @@
     if nx > 1:
         pl.when(ix < nx - 1)(v_halo(0).wait_send)
         pl.when(ix > 0)(v_halo(1).wait_send)
-    for copy, sends, _ in exchange:
-        pl.when(sends)(copy.wait_send)
+    for f in range(2):
+        for copy, sends, _ in exchange(f):
+            pl.when(sends)(copy.wait_send)
     pltpu.make_async_copy(many, many, ars_sem).wait()
 
 
@@ -560,8 +582,8 @@
             dma((peers, 2)),
             dma((2,)),
             dma((2,)),
-            dma((8,)),
-            dma((8,)),
+            dma((2, 8)),
+            dma((2, 8)),
             dma,
             dma,
             pltpu.SemaphoreType.REGULAR((5,)),

time: 21.6 us -> 21 us (0.972)
  Pallas kernels: 20.8 us -> 20.2 us
    pallas_call x1, Pallas kernels: 18.8 us -> 18.3 us  [shards(): pl.pallas_call(functools.partial(kernel, dims), out_shape=handed, in_spec...]
where the time goes in v3:
time: 21 us; the launch traced here: 20.9 us
  Pallas kernels  20.2 us (96%)
  between operations  0.64 us (3%)
    pallas_call x1, Pallas kernels, shards(): pl.pallas_call(functools.partial(kernel, dims), out_shape=handed, in_spec...  18.3 us
    pallas_call x1, Pallas kernels, shards(): pl.pallas_call(functools.partial(proximal, dims), out_shape=(block, block...  1.94 us

profile of v3, /device:TPU:0, one launch (start us, length us, event | category | flops | bytes accessed | tf_op | source)
XLA Modules:
  0.0 20.9 jit_solution(4093260122746925712)
XLA Ops:
  0.6 18.3 %shard_map.59 = (f32[544,128]{1,0:T(8,128)S(1)}, f32[544,128]{1,0:T(8,128)S(1)}, f32[19,16,128]{2,1,0:T(8,128)S(1)}, f32[1,128]{1,0:T(1,128)S(1)}) custom-call(f32[16,32,16,128]{3,2,1,0:T(8,128)} %partials.1, s32[32,32]{1,0:T(8,128)} %code_bits.1, s32[32]{0:T(128)} %group_map.1, f32[16,16,128]{2,1,0:T(8,128)} %velocity.1), custom_call_target="tpu_custom_call" | custom-call | tf_op jit(solution)/shard_map/pallas_call | solution.py:556
  18.9 1.9 %shard_map.60 = (f32[16,16,128]{2,1,0:T(8,128)}, f32[16,16,128]{2,1,0:T(8,128)}) custom-call(f32[544,128]{1,0:T(8,128)S(1)} %get-tuple-element.6.va, f32[544,128]{1,0:T(8,128)S(1)} %get-tuple-element.7.ga, f32[19,16,128]{2,1,0:T(8,128)S(1)} %get-tuple-element.8.gw, f32[1,128]{1,0:T(1,128)S(1)} %get-tuple-element.9.scale_in), custom_call_target="tpu_custom_call" | custom-call | tf_op jit(solution)/shard_map/pallas_call | solution.py:595
